TPU v7x, 512 devices: a whole 4x4x16 slice. The times are simulated.
512 devices in a mesh: row: 64 (over z, x), col: 8 (over y, core).
Axes of the slice: x: 4, y: 4, z: 16, core: 2. Of those that a mesh axis runs over, the one named last changes fastest.
Arguments:
- gate_up: bfloat16 [4, 2, 14336, 4096], P(None, None, 'row', 'col'), may hold values from -0.09375 to 0.09375
- down_weight: bfloat16 [4, 4096, 14336], P(None, 'row', 'col'), may hold values from -0.046875 to 0.046875
- query_output: bfloat16 [4, 2, 4096, 4096], P(None, None, 'row', 'col'), may hold values from -0.09375 to 0.09375
- probe_gate: bfloat16 [4, 2, 16, 4096], P(None, None, None, 'col'), may hold values from -6 to 6
- probe_down: bfloat16 [4, 16, 14336], P(None, None, 'col'), may hold values from -6 to 6
- probe_query: bfloat16 [4, 2, 16, 4096], P(None, None, None, 'col'), may hold values from -6 to 6
Outputs:
- vector_gate: float32 [4, 2, 16, 4096], P(None, None, None, 'col')
- vector_down: float32 [4, 16, 14336], P(None, None, 'col')
- vector_query: float32 [4, 2, 16, 4096], P(None, None, None, 'col')
- sigma_gate: float32 [4, 2, 16], replicated
- sigma_down: float32 [4, 16], replicated
- sigma_query: float32 [4, 2, 16], replicated
All inputs are finite; a program needn't handle non-finite values.
Results may differ from a plain program's by a relative error of at most 0.0033.
Values may be sent and summed in bfloat16 or wider, within the bound.
No kernel may reach another device: no remote copies, remote signals or barrier semaphores. Data moves between devices by JAX's collectives and lax.ppermute only.
A program may use at most 64 MiB of HBM per device.

v0:
```python
import jax
import jax.numpy as jnp
from jax import lax
from jax.sharding import Mesh
from jax.sharding import PartitionSpec as P

ITERS = 2
ROW = ("row_0", "row_1")
epsilon = 1e-06


def copy_for_each(shard, axis):
    length = lax.axis_size(axis)
    return lax.all_to_all(
        jnp.broadcast_to(shard[None], (length, *shard.shape)), axis, 0, 0, tiled=True
    )


def of_everyone(shard, axis):
    everything = copy_for_each(shard, axis)
    return jnp.sum(everything, axis=0)


def over_axes(shard, axes):
    for axis in axes:
        shard = lax.psum(shard, axis)
    return shard


def body(gate_up, down_weight, query_output, probe_gate, probe_down, probe_query):
    row_count = lax.axis_size(ROW)
    col_count = lax.axis_size("col")
    weights = (gate_up, down_weight[:, None], query_output)
    vectors = (probe_gate, probe_down[:, None], probe_query)
    scaled_right = vectors
    spectral = None

    def left_factor(total, weight):
        return lax.rsqrt(total[..., None] / (weight.shape[2] * row_count) + epsilon)

    for turn in range(ITERS):
        partial_value = tuple(
            (
                jnp.einsum("lmoi,lmki->lmko", weight, vector, preferred_element_type=jnp.float32)
                for weight, vector in zip(weights, vectors)
            )
        )
        summed = jax.tree.map(lambda part: of_everyone(part, "col"), partial_value)
        squares = tuple((jnp.sum(piece * piece, axis=3) for piece in summed))
        totals = jax.tree.map(lambda part: over_axes(part, ROW), squares)
        left_vecs = tuple((piece.astype(jnp.bfloat16) for piece in summed))
        right_partial = tuple(
            (
                jnp.einsum("lmoi,lmko->lmki", weight, left, preferred_element_type=jnp.float32)
                for weight, left in zip(weights, left_vecs)
            )
        )
        raw_sums = lax.psum(right_partial, ROW)
        right_sums = tuple(
            (
                raw * left_factor(total, weight)
                for raw, total, weight in zip(raw_sums, totals, weights)
            )
        )
        right_squares = tuple((jnp.sum(piece * piece, axis=3) for piece in right_sums))
        right_totals = jax.tree.map(lambda part: of_everyone(part, "col"), right_squares)
        scaled_right = tuple(
            (
                piece * lax.rsqrt(total[..., None] / (piece.shape[3] * col_count) + epsilon)
                for piece, total in zip(right_sums, right_totals)
            )
        )
        spectral = tuple(
            (
                jnp.sqrt(total / (weight.shape[2] * row_count))
                for weight, total in zip(weights, right_totals)
            )
        )
        vectors = tuple((piece.astype(jnp.bfloat16) for piece in scaled_right))
    return (
        scaled_right[0],
        scaled_right[1][:, 0],
        scaled_right[2],
        spectral[0],
        spectral[1][:, 0],
        spectral[2],
    )


def solution(mesh):
    finer = Mesh(mesh.devices.reshape(16, 4, mesh.shape["col"]), ("row_0", "row_1", "col"))
    in_specs = (
        P(None, None, ROW, "col"),
        P(None, ROW, "col"),
        P(None, None, ROW, "col"),
        P(None, None, None, "col"),
        P(None, None, "col"),
        P(None, None, None, "col"),
    )
    out_specs = (
        P(None, None, None, "col"),
        P(None, None, "col"),
        P(None, None, None, "col"),
        P(),
        P(),
        P(),
    )
    return jax.shard_map(body, mesh=finer, in_specs=in_specs, out_specs=out_specs, check_vma=False)
```

profile of v0, /device:TPU:1, one launch (start us, length us, event | category | flops | bytes accessed | tf_op | source)
XLA Modules:
  0.0 717.1 jit_solution(13803138326627123436)
XLA Ops:
  7.2 1.8 fusion.22
  9.9 10.1 %all-to-all-start.4 = ((f32[8,1,4096]{2,1,0:T(1,128)}), f32[8,1,4096]{2,1,0:T(1,128)S(1)}, u32[]{:S(2)}, u32[]{:S(2)}) async-start(f32[8,1,4096]{2,1,0:T(1,128)} %reshape.197), calls=%async_computation.4 | async-start | bytes 262144 | tf_op jit(solution)/shard_map/all_to_all | solution.py:14
  20.3 1.0 reshape.201
  21.3 3.9 all-to-all-done.4
  25.2 4.2 all-to-all-start.8
  29.4 1.2 fusion.21
  30.7 5.2 all-to-all-done.8
  35.9 2.2 broadcast_in_dim.24
  38.1 5.1 all-to-all-start
  43.7 2.4 reduce.10
  46.2 1.7 reshape.198
  47.9 1.6 reduce_sum.228
  49.4 1.8 convolution_bitcast_fusion.1
  51.2 2.1 reduce.11
  53.3 1.0 reshape.202
  54.4 1.1 reduce_sum.238
  55.5 0.9 fusion.17
  56.4 2.0 all-to-all-done
  58.3 1.3 reduce_sum.220
  59.7 1.1 fusion.13
  61.1 45.7 %all-reduce.3 = (f32[4,2,16]{2,1,0:T(2,128)S(1)}, f32[4,1,16]{2,0,1:T(4,128)S(1)}, f32[4,2,16]{2,1,0:T(2,128)S(1)}) all-reduce(f32[4,2,16]{2,1,0:T(2,128)S(1)} %multiply_reduce_fusion.7, f32[4,1,16]{2,0,1:T(4,128)S(1)} %bitcast.30, f32[4,2,16]{2,1,0:T(2,128)S(1)} %multiply_reduce_fusion.9), channel_id=1, replica_groups=mesh['row_0'=16,'row_1'=4,'col'=8] {'row_0'}, use_global_device_ids=true, to_apply=%region_3.0 | all-reduce | flops 320 | bytes 2560 | tf_op jit(solution)/shard_map/psum | solution.py:26
  106.7 13.6 %all-reduce.5 = (f32[4,2,16]{2,1,0:T(2,128)S(1)}, f32[4,1,16]{2,0,1:T(4,128)S(1)}, f32[4,2,16]{2,1,0:T(2,128)S(1)}) all-reduce(f32[4,2,16]{2,1,0:T(2,128)S(1)} %get-tuple-element.15, f32[4,1,16]{2,0,1:T(4,128)S(1)} %get-tuple-element.16, f32[4,2,16]{2,1,0:T(2,128)S(1)} %get-tuple-element.17), channel_id=1, replica_groups=mesh['row_0'=16,'row_1'=4,'col'=8] {'row_1'}, use_global_device_ids=true, to_apply=%region_4.0 | all-reduce | flops 320 | bytes 2560 | tf_op jit(solution)/shard_map/psum | solution.py:26
  120.3 203.2 %all-reduce.11.cloned.1.call-done = (f32[4,2,16,512]{3,2,1,0:T(8,128)}, f32[4,1,16,1792]{3,2,0,1:T(8,128)}, f32[4,2,16,512]{3,2,1,0:T(8,128)}) async-done(((f32[4,2,16,512]{3,2,1,0:T(8,128)}, f32[4,1,16,1792]{3,2,0,1:T(8,128)}, f32[4,2,16,512]{3,2,1,0:T(8,128)}), (f32[4,2,16,512]{3,2,1,0:T(8,128)}, f32[4,1,16,1792]{3,2,0,1:T(8,128)}, f32[4,2,16,512]{3,2,1,0:T(8,128)})) %all-reduce.11.cloned.1.call-update) | async-done | bytes 983056 | tf_op jit(solution)/shard_map/psum | solution.py:58
  323.6 1.2 multiply_reduce_fusion.1
  325.4 15.1 %all-to-all-start.5 = ((f32[8,4,1,16]{3,2,1,0:T(1,128)}), f32[8,4,1,16]{3,2,1,0:T(1,128)S(1)}, u32[]{:S(2)}, u32[]{:S(2)}) async-start(f32[8,4,1,16]{3,2,1,0:T(1,128)} %broadcast_in_dim.29), calls=%async_computation.5 | async-start | bytes 32768 | tf_op jit(solution)/shard_map/all_to_all | solution.py:14
  340.5 1.1 multiply_reduce_fusion.3
  341.6 1.1 multiply_reduce_fusion.5
  344.2 1.0 all-to-all-done.5
  345.1 3.9 all-to-all-start.9
  349.1 1.4 fusion.1
  351.3 1.8 reshape.199
  354.2 4.3 all-to-all-start.1
  358.5 1.3 reduce.14
  361.3 1.2 fusion.6
  362.5 0.9 broadcast_in_dim.34
  363.4 2.1 reshape.205
  365.5 4.8 all-to-all-start.6
  372.4 3.3 all-to-all-done.6
  375.6 4.8 all-to-all-start.10
  380.4 1.3 fusion.5
  381.7 5.3 all-to-all-done.10
  387.0 2.1 broadcast_in_dim.26
  389.1 5.1 all-to-all-start.2
  394.2 2.4 reduce.13
  396.7 1.0 reshape.200
  398.3 1.8 convolution_bitcast_fusion
  400.1 2.1 reduce.15
  402.5 0.9 fusion.15
  403.4 6.0 all-to-all-done.2
  409.3 1.3 reduce_sum.224
  410.7 1.1 fusion.11
  412.1 41.4 %all-reduce.2 = (f32[4,2,16]{2,1,0:T(2,128)S(1)}, f32[4,1,16]{2,0,1:T(4,128)S(1)}, f32[4,2,16]{2,1,0:T(2,128)S(1)}) all-reduce(f32[4,2,16]{2,1,0:T(2,128)S(1)} %multiply_reduce_fusion.6, f32[4,1,16]{2,0,1:T(4,128)S(1)} %bitcast.31, f32[4,2,16]{2,1,0:T(2,128)S(1)} %multiply_reduce_fusion.8), channel_id=1, replica_groups=mesh['row_0'=16,'row_1'=4,'col'=8] {'row_0'}, use_global_device_ids=true, to_apply=%region_10.0 | all-reduce | flops 320 | bytes 2560 | tf_op jit(solution)/shard_map/psum | solution.py:26
  453.4 13.0 %all-reduce.4 = (f32[4,2,16]{2,1,0:T(2,128)S(1)}, f32[4,1,16]{2,0,1:T(4,128)S(1)}, f32[4,2,16]{2,1,0:T(2,128)S(1)}) all-reduce(f32[4,2,16]{2,1,0:T(2,128)S(1)} %get-tuple-element.12, f32[4,1,16]{2,0,1:T(4,128)S(1)} %get-tuple-element.13, f32[4,2,16]{2,1,0:T(2,128)S(1)} %get-tuple-element.14), channel_id=1, replica_groups=mesh['row_0'=16,'row_1'=4,'col'=8] {'row_1'}, use_global_device_ids=true, to_apply=%region_11.0 | all-reduce | flops 320 | bytes 2560 | tf_op jit(solution)/shard_map/psum | solution.py:26
  466.4 203.1 %all-reduce.9.cloned.1.call-done = (f32[4,2,16,512]{3,2,1,0:T(8,128)}, f32[4,1,16,1792]{3,2,0,1:T(8,128)}, f32[4,2,16,512]{3,2,1,0:T(8,128)}) async-done(((f32[4,2,16,512]{3,2,1,0:T(8,128)}, f32[4,1,16,1792]{3,2,0,1:T(8,128)}, f32[4,2,16,512]{3,2,1,0:T(8,128)}), (f32[4,2,16,512]{3,2,1,0:T(8,128)}, f32[4,1,16,1792]{3,2,0,1:T(8,128)}, f32[4,2,16,512]{3,2,1,0:T(8,128)})) %all-reduce.9.cloned.1.call-update) | async-done | bytes 983056 | tf_op jit(solution)/shard_map/psum | solution.py:58
  669.6 1.3 multiply_reduce_fusion
  671.5 15.1 %all-to-all-start.7 = ((f32[8,4,1,16]{3,2,1,0:T(1,128)}), f32[8,4,1,16]{3,2,1,0:T(1,128)S(1)}, u32[]{:S(2)}, u32[]{:S(2)}) async-start(f32[8,4,1,16]{3,2,1,0:T(1,128)} %broadcast_in_dim.31), calls=%async_computation.7 | async-start | bytes 32768 | tf_op jit(solution)/shard_map/all_to_all | solution.py:14
  686.5 1.1 multiply_reduce_fusion.2
  687.7 1.1 multiply_reduce_fusion.4
  690.2 1.0 all-to-all-done.7
  691.2 3.9 all-to-all-start.11
  695.7 1.9 multiply_bitcast_fusion
  697.6 2.0 all-to-all-done.11
  699.7 3.9 all-to-all-start.3
  705.7 2.4 all-to-all-done.3
  (83 shorter events, 17.7 us)
Async XLA Ops:
  7.2 22.3 %copy-start = (bf16[4,2,224,512]{3,2,1,0:T(8,128)(2,1)S(1)}, bf16[4,2,224,512]{3,2,1,0:T(8,128)(2,1)}, u32[]{:S(2)}) copy-start(bf16[4,2,224,512]{3,2,1,0:T(8,128)(2,1)} %param.6) | copy-start | bytes 5505028
  7.2 12.8 %copy-start.11 = (bf16[4,2,16,512]{3,2,1,0:T(8,128)(2,1)S(1)}, bf16[4,2,16,512]{3,2,1,0:T(8,128)(2,1)}, u32[]{:S(2)}) copy-start(bf16[4,2,16,512]{3,2,1,0:T(8,128)(2,1)} %param.11) | copy-start | bytes 393220
  7.2 12.8 %copy-start.2 = (bf16[4,2,64,512]{3,2,1,0:T(8,128)(2,1)S(1)}, bf16[4,2,64,512]{3,2,1,0:T(8,128)(2,1)}, u32[]{:S(2)}) copy-start(bf16[4,2,64,512]{3,2,1,0:T(8,128)(2,1)} %param.8) | copy-start | bytes 1572868
  9.0 20.4 %copy-start.10 = (bf16[4,2,16,512]{3,2,1,0:T(8,128)(2,1)S(1)}, bf16[4,2,16,512]{3,2,1,0:T(8,128)(2,1)}, u32[]{:S(2)}) copy-start(bf16[4,2,16,512]{3,2,1,0:T(8,128)(2,1)} %param.9) | copy-start | bytes 393220
  9.9 15.4 %all-to-all-start.4 = ((f32[8,1,4096]{2,1,0:T(1,128)}), f32[8,1,4096]{2,1,0:T(1,128)S(1)}, u32[]{:S(2)}, u32[]{:S(2)}) async-start(f32[8,1,4096]{2,1,0:T(1,128)} %reshape.197), calls=%async_computation.4 | async-start | bytes 262144 | tf_op jit(solution)/shard_map/all_to_all | solution.py:14
  25.2 4.2 copy-start.7
  25.2 10.7 %all-to-all-start.8 = ((f32[8,1,8192]{2,1,0:T(1,128)}), f32[8,1,8192]{2,1,0:T(1,128)S(1)}, u32[]{:S(2)}, u32[]{:S(2)}) async-start(f32[8,1,8192]{2,1,0:T(1,128)} %reshape.201), calls=%async_computation.8 | async-start | bytes 524288 | tf_op jit(solution)/shard_map/all_to_all | solution.py:14
  30.7 18.8 %copy-start.1 = (bf16[4,64,1792]{2,1,0:T(8,128)(2,1)S(1)}, bf16[4,64,1792]{2,1,0:T(8,128)(2,1)}, u32[]{:S(2)}) copy-start(bf16[4,64,1792]{2,1,0:T(8,128)(2,1)} %param.7) | copy-start | bytes 2752516
  35.9 12.0 %copy-start.4 = (f32[8,1,8192]{2,1,0:T(1,128)}, f32[8,1,8192]{2,1,0:T(1,128)S(1)}, u32[]{:S(2)}) copy-start(f32[8,1,8192]{2,1,0:T(1,128)S(1)} %all-to-all-done.8) | copy-start | bytes 786436
  38.1 20.2 %all-to-all-start = ((f32[8,4,2,16,224]{4,3,2,1,0:T(8,128)}), f32[8,4,2,16,224]{4,3,2,1,0:T(8,128)}, u32[]{:S(2)}, u32[]{:S(2)}) async-start(f32[8,4,2,16,224]{4,3,2,1,0:T(8,128)} %broadcast_in_dim.24), calls=%async_computation | async-start | bytes 2097152 | tf_op jit(solution)/shard_map/all_to_all | solution.py:14
  43.2 280.4 %all-reduce.11.cloned.1.call-start = ((), (), s32[]{:S(2)}) async-start(), calls=%async_computation.13 | async-start | bytes 1966080 | tf_op jit(solution)/shard_map/psum | solution.py:58
  59.7 1.1 copy-start.8
  325.4 19.7 %all-to-all-start.5 = ((f32[8,4,1,16]{3,2,1,0:T(1,128)}), f32[8,4,1,16]{3,2,1,0:T(1,128)S(1)}, u32[]{:S(2)}, u32[]{:S(2)}) async-start(f32[8,4,1,16]{3,2,1,0:T(1,128)} %broadcast_in_dim.29), calls=%async_computation.5 | async-start | bytes 32768 | tf_op jit(solution)/shard_map/all_to_all | solution.py:14
  345.1 8.5 %all-to-all-start.9 = ((f32[8,1,128]{2,1,0:T(1,128)}), f32[8,1,128]{2,1,0:T(1,128)S(1)}, u32[]{:S(2)}, u32[]{:S(2)}) async-start(f32[8,1,128]{2,1,0:T(1,128)} %reshape.203), calls=%async_computation.9 | async-start | bytes 8192 | tf_op jit(solution)/shard_map/all_to_all | solution.py:14
  351.3 29.1 %copy-start.3 = (f32[4,2,16,512]{3,2,1,0:T(8,128)S(1)}, f32[4,2,16,512]{3,2,1,0:T(8,128)}, u32[]{:S(2)}) copy-start(f32[4,2,16,512]{3,2,1,0:T(8,128)} %get-tuple-element.9) | copy-start | bytes 786436
  353.6 0.6 copy-start.12
  354.2 11.3 %all-to-all-start.1 = ((f32[8,1,128]{2,1,0:T(1,128)}), f32[8,1,128]{2,1,0:T(1,128)S(1)}, u32[]{:S(2)}, u32[]{:S(2)}) async-start(f32[8,1,128]{2,1,0:T(1,128)} %reshape.193), calls=%async_computation.1 | async-start | bytes 8192 | tf_op jit(solution)/shard_map/all_to_all | solution.py:14
  365.5 10.2 %all-to-all-start.6 = ((f32[8,1,4096]{2,1,0:T(1,128)}), f32[8,1,4096]{2,1,0:T(1,128)}, u32[]{:S(2)}, u32[]{:S(2)}) async-start(f32[8,1,4096]{2,1,0:T(1,128)} %reshape.199), calls=%async_computation.6 | async-start | bytes 262144 | tf_op jit(solution)/shard_map/all_to_all | solution.py:14
  375.6 11.4 %all-to-all-start.10 = ((f32[8,1,8192]{2,1,0:T(1,128)}), f32[8,1,8192]{2,1,0:T(1,128)}, u32[]{:S(2)}, u32[]{:S(2)}) async-start(f32[8,1,8192]{2,1,0:T(1,128)} %reshape.205), calls=%async_computation.10 | async-start | bytes 524288 | tf_op jit(solution)/shard_map/all_to_all | solution.py:14
  389.1 20.2 %all-to-all-start.2 = ((f32[8,4,2,16,224]{4,3,2,1,0:T(8,128)}), f32[8,4,2,16,224]{4,3,2,1,0:T(8,128)}, u32[]{:S(2)}, u32[]{:S(2)}) async-start(f32[8,4,2,16,224]{4,3,2,1,0:T(8,128)} %broadcast_in_dim.26), calls=%async_computation.2 | async-start | bytes 2097152 | tf_op jit(solution)/shard_map/all_to_all | solution.py:14
  394.2 275.3 %all-reduce.9.cloned.1.call-start = ((), (), s32[]{:S(2)}) async-start(), calls=%async_computation.12 | async-start | bytes 1966080 | tf_op jit(solution)/shard_map/psum | solution.py:58
  410.7 1.1 copy-start.9
  669.6 35.3 %copy-start.6 = (f32[4,2,16,512]{3,2,1,0:T(8,128)S(1)}, f32[4,2,16,512]{3,2,1,0:T(8,128)}, u32[]{:S(2)}) copy-start(f32[4,2,16,512]{3,2,1,0:T(8,128)} %get-tuple-element.8) | copy-start | bytes 786436
  669.6 39.9 %copy-start.5 = (f32[4,2,16,512]{3,2,1,0:T(8,128)S(1)}, f32[4,2,16,512]{3,2,1,0:T(8,128)}, u32[]{:S(2)}) copy-start(f32[4,2,16,512]{3,2,1,0:T(8,128)} %get-tuple-element.6) | copy-start | bytes 786436
  671.5 19.7 %all-to-all-start.7 = ((f32[8,4,1,16]{3,2,1,0:T(1,128)}), f32[8,4,1,16]{3,2,1,0:T(1,128)S(1)}, u32[]{:S(2)}, u32[]{:S(2)}) async-start(f32[8,4,1,16]{3,2,1,0:T(1,128)} %broadcast_in_dim.31), calls=%async_computation.7 | async-start | bytes 32768 | tf_op jit(solution)/shard_map/all_to_all | solution.py:14
  691.2 8.5 %all-to-all-start.11 = ((f32[8,1,128]{2,1,0:T(1,128)}), f32[8,1,128]{2,1,0:T(1,128)S(1)}, u32[]{:S(2)}, u32[]{:S(2)}) async-start(f32[8,1,128]{2,1,0:T(1,128)} %reshape.207), calls=%async_computation.11 | async-start | bytes 8192 | tf_op jit(solution)/shard_map/all_to_all | solution.py:14
  699.7 8.5 %all-to-all-start.3 = ((f32[8,1,128]{2,1,0:T(1,128)}), f32[8,1,128]{2,1,0:T(1,128)S(1)}, u32[]{:S(2)}, u32[]{:S(2)}) async-start(f32[8,1,128]{2,1,0:T(1,128)} %reshape.195), calls=%async_computation.3 | async-start | bytes 8192 | tf_op jit(solution)/shard_map/all_to_all | solution.py:14
Sparse Core Ops, SparseCore 0:
  60.9 262.6 all-reduce.10
  411.9 257.6 all-reduce.8
where the time goes:
time: 719 us; the launch traced here: 717 us
  waiting for transfers between devices  439 us (61%)
  blocking collectives  114 us (16%)
  starting transfers between devices  80.4 us (11%)
  other arithmetic  32.7 us (5%)
  local copies, waits for them, and re-layouts  22.5 us (3%)
  matrix products  14.6 us (2%)
  between operations  14.3 us (2%)
    psum x2, waiting for transfers between devices, body(): raw_sums = lax.psum(right_partial, ROW)  406 us
    psum x4, blocking collectives, over_axes(): shard = lax.psum(shard, axis)  114 us
    all_to_all x12, starting transfers between devices, copy_for_each(): lax.all_to_all(jnp.broadcast_to(shard[None], (length, *shard.shape)), axi...  80.4 us
    all_to_all x12, waiting for transfers between devices, copy_for_each(): lax.all_to_all(jnp.broadcast_to(shard[None], (length, *shard.shape)), axi...  32.5 us
    unnamed x42, local copies, waits for them, and re-layouts  14.8 us
  transfers between devices with their start and end apart: 14, of which 13 were waited for; matrix products, arithmetic and copies ran while one was open for 7% of the time, Pallas kernels for 0%

commit v1 on v0

--- a/solution.py
+++ b/solution.py
@@ -55,7 +55,8 @@
                 for weight, left in zip(weights, left_vecs)
             )
         )
-        raw_sums = lax.psum(right_partial, ROW)
+        half = lax.psum(right_partial, "row_1")
+        raw_sums = lax.psum(half, "row_0")
         right_sums = tuple(
             (
                 raw * left_factor(total, weight)

time: 719 us -> 581 us (0.81)
  waiting for transfers between devices: 439 us -> 300 us
    psum x2 -> x4, waiting for transfers between devices: 406 us -> 267 us  [the longest x2 155 us: body(): raw_sums = lax.psum(half, 'row_0')]
  transfers between devices with their start and end apart: 14 -> 16, of which waited for: 13 -> 15; matrix products, arithmetic and copies ran while one was open for 7% -> 9% of each run, Pallas kernels for 0% -> 0%
where the time goes in v1:
time: 581 us; the launch traced here: 579 us
  waiting for transfers between devices  300 us (52%)
  blocking collectives  115 us (20%)
  starting transfers between devices  79.4 us (14%)
  other arithmetic  32.7 us (6%)
  local copies, waits for them, and re-layouts  22.5 us (4%)
  matrix products  14.6 us (3%)
  between operations  14 us (2%)
    psum x2, waiting for transfers between devices, body(): raw_sums = lax.psum(half, 'row_0')  155 us
    psum x4, blocking collectives, over_axes(): shard = lax.psum(shard, axis)  115 us
    psum x2, waiting for transfers between devices, body(): half = lax.psum(right_partial, 'row_1')  112 us
    all_to_all x12, starting transfers between devices, copy_for_each(): lax.all_to_all(jnp.broadcast_to(shard[None], (length, *shard.shape)), axi...  79.3 us
    all_to_all x12, waiting for transfers between devices, copy_for_each(): lax.all_to_all(jnp.broadcast_to(shard[None], (length, *shard.shape)), axi...  32.5 us
    unnamed x42, local copies, waits for them, and re-layouts  14.8 us
    all_to_all x8, other arithmetic, copy_for_each(): lax.all_to_all(jnp.broadcast_to(shard[None], (length, *shard.shape)), axi...  12.1 us
  transfers between devices with their start and end apart: 16, of which 15 were waited for; matrix products, arithmetic and copies ran while one was open for 9% of the time, Pallas kernels for 0%

profile of v1, /device:TPU:1, one launch (start us, length us, event | category | flops | bytes accessed | tf_op | source)
XLA Modules:
  0.0 578.7 jit_solution(8544331438257606731)
XLA Ops:
  7.2 1.8 fusion.22
  9.9 10.1 %all-to-all-start.4 = ((f32[8,1,4096]{2,1,0:T(1,128)}), f32[8,1,4096]{2,1,0:T(1,128)S(1)}, u32[]{:S(2)}, u32[]{:S(2)}) async-start(f32[8,1,4096]{2,1,0:T(1,128)} %reshape.197), calls=%async_computation.4 | async-start | bytes 262144 | tf_op jit(solution)/shard_map/all_to_all | solution.py:14
  20.3 1.0 reshape.201
  21.3 3.9 all-to-all-done.4
  25.2 4.2 all-to-all-start.8
  29.4 1.2 fusion.21
  30.7 5.2 all-to-all-done.8
  35.9 2.2 broadcast_in_dim.24
  38.1 5.1 all-to-all-start
  43.7 2.4 reduce.10
  46.2 1.7 reshape.198
  47.9 1.6 reduce_sum.228
  49.4 1.8 convolution_bitcast_fusion.1
  51.2 2.1 reduce.11
  53.3 1.0 reshape.202
  54.4 1.1 reduce_sum.238
  55.5 0.9 fusion.17
  56.4 2.0 all-to-all-done
  58.3 1.3 reduce_sum.220
  59.7 1.1 fusion.13
  60.8 58.0 %all-reduce.19.cloned.1.call-done = (f32[4,2,16,512]{3,2,1,0:T(8,128)}, f32[4,1,16,1792]{3,2,0,1:T(8,128)}, f32[4,2,16,512]{3,2,1,0:T(8,128)}) async-done(((f32[4,2,16,512]{3,2,1,0:T(8,128)}, f32[4,1,16,1792]{3,2,0,1:T(8,128)}, f32[4,2,16,512]{3,2,1,0:T(8,128)}), (f32[4,2,16,512]{3,2,1,0:T(8,128)}, f32[4,1,16,1792]{3,2,0,1:T(8,128)}, f32[4,2,16,512]{3,2,1,0:T(8,128)})) %all-reduce.19.cloned.1.call-update) | async-done | bytes 983056 | tf_op jit(solution)/shard_map/psum | solution.py:58
  119.1 44.1 %all-reduce.1 = (f32[4,2,16]{2,1,0:T(2,128)S(1)}, f32[4,1,16]{2,0,1:T(4,128)S(1)}, f32[4,2,16]{2,1,0:T(2,128)S(1)}) all-reduce(f32[4,2,16]{2,1,0:T(2,128)S(1)} %multiply_reduce_fusion.7, f32[4,1,16]{2,0,1:T(4,128)S(1)} %bitcast.30, f32[4,2,16]{2,1,0:T(2,128)S(1)} %multiply_reduce_fusion.9), channel_id=1, replica_groups=mesh['row_0'=16,'row_1'=4,'col'=8] {'row_0'}, use_global_device_ids=true, to_apply=%region_4.0 | all-reduce | flops 320 | bytes 2560 | tf_op jit(solution)/shard_map/psum | solution.py:26
  163.2 13.8 %all-reduce.5 = (f32[4,2,16]{2,1,0:T(2,128)S(1)}, f32[4,1,16]{2,0,1:T(4,128)S(1)}, f32[4,2,16]{2,1,0:T(2,128)S(1)}) all-reduce(f32[4,2,16]{2,1,0:T(2,128)S(1)} %get-tuple-element.9, f32[4,1,16]{2,0,1:T(4,128)S(1)} %get-tuple-element.10, f32[4,2,16]{2,1,0:T(2,128)S(1)} %get-tuple-element.11), channel_id=1, replica_groups=mesh['row_0'=16,'row_1'=4,'col'=8] {'row_1'}, use_global_device_ids=true, to_apply=%region_5.0 | all-reduce | flops 320 | bytes 2560 | tf_op jit(solution)/shard_map/psum | solution.py:26
  177.1 77.6 %all-reduce.15.cloned.1.call-done = (f32[4,2,16,512]{3,2,1,0:T(8,128)}, f32[4,1,16,1792]{3,2,0,1:T(8,128)}, f32[4,2,16,512]{3,2,1,0:T(8,128)}) async-done(((f32[4,2,16,512]{3,2,1,0:T(8,128)}, f32[4,1,16,1792]{3,2,0,1:T(8,128)}, f32[4,2,16,512]{3,2,1,0:T(8,128)}), (f32[4,2,16,512]{3,2,1,0:T(8,128)}, f32[4,1,16,1792]{3,2,0,1:T(8,128)}, f32[4,2,16,512]{3,2,1,0:T(8,128)})) %all-reduce.15.cloned.1.call-update) | async-done | bytes 983056 | tf_op jit(solution)/shard_map/psum | solution.py:59
  254.6 1.2 multiply_reduce_fusion.1
  256.5 14.5 %all-to-all-start.5 = ((f32[8,4,1,16]{3,2,1,0:T(1,128)}), f32[8,4,1,16]{3,2,1,0:T(1,128)S(1)}, u32[]{:S(2)}, u32[]{:S(2)}) async-start(f32[8,4,1,16]{3,2,1,0:T(1,128)} %broadcast_in_dim.29), calls=%async_computation.5 | async-start | bytes 32768 | tf_op jit(solution)/shard_map/all_to_all | solution.py:14
  271.0 1.1 multiply_reduce_fusion.3
  272.1 1.1 multiply_reduce_fusion.5
  274.7 1.0 all-to-all-done.5
  275.7 3.9 all-to-all-start.9
  279.6 1.4 fusion.1
  281.8 1.8 reshape.199
  284.7 4.3 all-to-all-start.1
  289.0 1.3 reduce.14
  291.8 1.2 fusion.6
  293.9 2.1 reshape.205
  296.0 4.8 all-to-all-start.6
  302.9 3.3 all-to-all-done.6
  306.2 4.8 all-to-all-start.10
  310.9 1.3 fusion.5
  312.2 5.3 all-to-all-done.10
  317.5 2.1 broadcast_in_dim.26
  319.6 5.1 all-to-all-start.2
  324.7 2.4 reduce.13
  327.2 1.0 reshape.200
  328.8 1.8 convolution_bitcast_fusion
  330.6 2.1 reduce.15
  333.9 6.0 %all-to-all-done.2 = f32[8,4,2,16,224]{4,3,2,1,0:T(8,128)} async-done(((f32[8,4,2,16,224]{4,3,2,1,0:T(8,128)}), f32[8,4,2,16,224]{4,3,2,1,0:T(8,128)}, u32[]{:S(2)}, u32[]{:S(2)}) %all-to-all-start.2) | async-done | bytes 917536 | tf_op jit(solution)/shard_map/all_to_all | solution.py:14
  339.8 1.3 reduce_sum.224
  341.2 1.1 fusion.11
  342.3 54.0 %all-reduce.17.cloned.1.call-done = (f32[4,2,16,512]{3,2,1,0:T(8,128)}, f32[4,1,16,1792]{3,2,0,1:T(8,128)}, f32[4,2,16,512]{3,2,1,0:T(8,128)}) async-done(((f32[4,2,16,512]{3,2,1,0:T(8,128)}, f32[4,1,16,1792]{3,2,0,1:T(8,128)}, f32[4,2,16,512]{3,2,1,0:T(8,128)}), (f32[4,2,16,512]{3,2,1,0:T(8,128)}, f32[4,1,16,1792]{3,2,0,1:T(8,128)}, f32[4,2,16,512]{3,2,1,0:T(8,128)})) %all-reduce.17.cloned.1.call-update) | async-done | bytes 983056 | tf_op jit(solution)/shard_map/psum | solution.py:58
  396.7 44.0 %all-reduce = (f32[4,2,16]{2,1,0:T(2,128)S(1)}, f32[4,1,16]{2,0,1:T(4,128)S(1)}, f32[4,2,16]{2,1,0:T(2,128)S(1)}) all-reduce(f32[4,2,16]{2,1,0:T(2,128)S(1)} %multiply_reduce_fusion.6, f32[4,1,16]{2,0,1:T(4,128)S(1)} %bitcast.31, f32[4,2,16]{2,1,0:T(2,128)S(1)} %multiply_reduce_fusion.8), channel_id=1, replica_groups=mesh['row_0'=16,'row_1'=4,'col'=8] {'row_0'}, use_global_device_ids=true, to_apply=%region_12.0 | all-reduce | flops 320 | bytes 2560 | tf_op jit(solution)/shard_map/psum | solution.py:26
  440.7 13.5 %all-reduce.4 = (f32[4,2,16]{2,1,0:T(2,128)S(1)}, f32[4,1,16]{2,0,1:T(4,128)S(1)}, f32[4,2,16]{2,1,0:T(2,128)S(1)}) all-reduce(f32[4,2,16]{2,1,0:T(2,128)S(1)} %get-tuple-element.6, f32[4,1,16]{2,0,1:T(4,128)S(1)} %get-tuple-element.7, f32[4,2,16]{2,1,0:T(2,128)S(1)} %get-tuple-element.8), channel_id=1, replica_groups=mesh['row_0'=16,'row_1'=4,'col'=8] {'row_1'}, use_global_device_ids=true, to_apply=%region_13.0 | all-reduce | flops 320 | bytes 2560 | tf_op jit(solution)/shard_map/psum | solution.py:26
  454.3 77.8 %all-reduce.13.cloned.1.call-done = (f32[4,2,16,512]{3,2,1,0:T(8,128)}, f32[4,1,16,1792]{3,2,0,1:T(8,128)}, f32[4,2,16,512]{3,2,1,0:T(8,128)}) async-done(((f32[4,2,16,512]{3,2,1,0:T(8,128)}, f32[4,1,16,1792]{3,2,0,1:T(8,128)}, f32[4,2,16,512]{3,2,1,0:T(8,128)}), (f32[4,2,16,512]{3,2,1,0:T(8,128)}, f32[4,1,16,1792]{3,2,0,1:T(8,128)}, f32[4,2,16,512]{3,2,1,0:T(8,128)})) %all-reduce.13.cloned.1.call-update) | async-done | bytes 983056 | tf_op jit(solution)/shard_map/psum | solution.py:59
  532.0 1.3 multiply_reduce_fusion
  533.9 14.5 %all-to-all-start.7 = ((f32[8,4,1,16]{3,2,1,0:T(1,128)}), f32[8,4,1,16]{3,2,1,0:T(1,128)S(1)}, u32[]{:S(2)}, u32[]{:S(2)}) async-start(f32[8,4,1,16]{3,2,1,0:T(1,128)} %broadcast_in_dim.31), calls=%async_computation.7 | async-start | bytes 32768 | tf_op jit(solution)/shard_map/all_to_all | solution.py:14
  548.5 1.1 multiply_reduce_fusion.2
  549.6 1.1 multiply_reduce_fusion.4
  552.2 1.0 all-to-all-done.7
  553.1 3.9 all-to-all-start.11
  557.7 1.9 multiply_bitcast_fusion
  559.6 2.0 all-to-all-done.11
  561.6 3.9 all-to-all-start.3
  567.6 2.4 all-to-all-done.3
  (89 shorter events, 19.6 us)
Async XLA Ops:
  7.2 22.3 %copy-start = (bf16[4,2,224,512]{3,2,1,0:T(8,128)(2,1)S(1)}, bf16[4,2,224,512]{3,2,1,0:T(8,128)(2,1)}, u32[]{:S(2)}) copy-start(bf16[4,2,224,512]{3,2,1,0:T(8,128)(2,1)} %param.6) | copy-start | bytes 5505028
  7.2 12.8 %copy-start.11 = (bf16[4,2,16,512]{3,2,1,0:T(8,128)(2,1)S(1)}, bf16[4,2,16,512]{3,2,1,0:T(8,128)(2,1)}, u32[]{:S(2)}) copy-start(bf16[4,2,16,512]{3,2,1,0:T(8,128)(2,1)} %param.11) | copy-start | bytes 393220
  7.2 12.8 %copy-start.2 = (bf16[4,2,64,512]{3,2,1,0:T(8,128)(2,1)S(1)}, bf16[4,2,64,512]{3,2,1,0:T(8,128)(2,1)}, u32[]{:S(2)}) copy-start(bf16[4,2,64,512]{3,2,1,0:T(8,128)(2,1)} %param.8) | copy-start | bytes 1572868
  9.0 20.4 %copy-start.10 = (bf16[4,2,16,512]{3,2,1,0:T(8,128)(2,1)S(1)}, bf16[4,2,16,512]{3,2,1,0:T(8,128)(2,1)}, u32[]{:S(2)}) copy-start(bf16[4,2,16,512]{3,2,1,0:T(8,128)(2,1)} %param.9) | copy-start | bytes 393220
  9.9 15.4 %all-to-all-start.4 = ((f32[8,1,4096]{2,1,0:T(1,128)}), f32[8,1,4096]{2,1,0:T(1,128)S(1)}, u32[]{:S(2)}, u32[]{:S(2)}) async-start(f32[8,1,4096]{2,1,0:T(1,128)} %reshape.197), calls=%async_computation.4 | async-start | bytes 262144 | tf_op jit(solution)/shard_map/all_to_all | solution.py:14
  25.2 4.2 copy-start.7
  25.2 10.7 %all-to-all-start.8 = ((f32[8,1,8192]{2,1,0:T(1,128)}), f32[8,1,8192]{2,1,0:T(1,128)S(1)}, u32[]{:S(2)}, u32[]{:S(2)}) async-start(f32[8,1,8192]{2,1,0:T(1,128)} %reshape.201), calls=%async_computation.8 | async-start | bytes 524288 | tf_op jit(solution)/shard_map/all_to_all | solution.py:14
  30.7 18.8 %copy-start.1 = (bf16[4,64,1792]{2,1,0:T(8,128)(2,1)S(1)}, bf16[4,64,1792]{2,1,0:T(8,128)(2,1)}, u32[]{:S(2)}) copy-start(bf16[4,64,1792]{2,1,0:T(8,128)(2,1)} %param.7) | copy-start | bytes 2752516
  35.9 12.0 %copy-start.4 = (f32[8,1,8192]{2,1,0:T(1,128)}, f32[8,1,8192]{2,1,0:T(1,128)S(1)}, u32[]{:S(2)}) copy-start(f32[8,1,8192]{2,1,0:T(1,128)S(1)} %all-to-all-done.8) | copy-start | bytes 786436
  38.1 20.2 %all-to-all-start = ((f32[8,4,2,16,224]{4,3,2,1,0:T(8,128)}), f32[8,4,2,16,224]{4,3,2,1,0:T(8,128)}, u32[]{:S(2)}, u32[]{:S(2)}) async-start(f32[8,4,2,16,224]{4,3,2,1,0:T(8,128)} %broadcast_in_dim.24), calls=%async_computation | async-start | bytes 2097152 | tf_op jit(solution)/shard_map/all_to_all | solution.py:14
  43.2 75.6 %all-reduce.19.cloned.1.call-start = ((), (), s32[]{:S(2)}) async-start(), calls=%async_computation.15 | async-start | bytes 1966080 | tf_op jit(solution)/shard_map/psum | solution.py:58
  59.7 59.1 %copy-start.8 = (f32[4,16,64]{2,1,0:T(8,128)S(1)}, f32[4,16,64]{2,1,0:T(8,128)}, u32[]{:S(2)}) copy-start(f32[4,16,64]{2,1,0:T(8,128)} %reduce_sum.228) | copy-start | bytes 49156
  60.7 193.9 %all-reduce.15.cloned.1.call-start = ((), (), s32[]{:S(2)}) async-start(), calls=%async_computation.13 | async-start | bytes 1966080 | tf_op jit(solution)/shard_map/psum | solution.py:59
  256.5 19.2 %all-to-all-start.5 = ((f32[8,4,1,16]{3,2,1,0:T(1,128)}), f32[8,4,1,16]{3,2,1,0:T(1,128)S(1)}, u32[]{:S(2)}, u32[]{:S(2)}) async-start(f32[8,4,1,16]{3,2,1,0:T(1,128)} %broadcast_in_dim.29), calls=%async_computation.5 | async-start | bytes 32768 | tf_op jit(solution)/shard_map/all_to_all | solution.py:14
  275.7 8.5 %all-to-all-start.9 = ((f32[8,1,128]{2,1,0:T(1,128)}), f32[8,1,128]{2,1,0:T(1,128)S(1)}, u32[]{:S(2)}, u32[]{:S(2)}) async-start(f32[8,1,128]{2,1,0:T(1,128)} %reshape.203), calls=%async_computation.9 | async-start | bytes 8192 | tf_op jit(solution)/shard_map/all_to_all | solution.py:14
  281.8 29.1 %copy-start.3 = (f32[4,2,16,512]{3,2,1,0:T(8,128)S(1)}, f32[4,2,16,512]{3,2,1,0:T(8,128)}, u32[]{:S(2)}) copy-start(f32[4,2,16,512]{3,2,1,0:T(8,128)} %get-tuple-element.15) | copy-start | bytes 786436
  284.1 0.6 copy-start.12
  284.7 11.3 %all-to-all-start.1 = ((f32[8,1,128]{2,1,0:T(1,128)}), f32[8,1,128]{2,1,0:T(1,128)S(1)}, u32[]{:S(2)}, u32[]{:S(2)}) async-start(f32[8,1,128]{2,1,0:T(1,128)} %reshape.193), calls=%async_computation.1 | async-start | bytes 8192 | tf_op jit(solution)/shard_map/all_to_all | solution.py:14
  296.0 10.2 %all-to-all-start.6 = ((f32[8,1,4096]{2,1,0:T(1,128)}), f32[8,1,4096]{2,1,0:T(1,128)}, u32[]{:S(2)}, u32[]{:S(2)}) async-start(f32[8,1,4096]{2,1,0:T(1,128)} %reshape.199), calls=%async_computation.6 | async-start | bytes 262144 | tf_op jit(solution)/shard_map/all_to_all | solution.py:14
  306.2 11.4 %all-to-all-start.10 = ((f32[8,1,8192]{2,1,0:T(1,128)}), f32[8,1,8192]{2,1,0:T(1,128)}, u32[]{:S(2)}, u32[]{:S(2)}) async-start(f32[8,1,8192]{2,1,0:T(1,128)} %reshape.205), calls=%async_computation.10 | async-start | bytes 524288 | tf_op jit(solution)/shard_map/all_to_all | solution.py:14
  319.6 20.2 %all-to-all-start.2 = ((f32[8,4,2,16,224]{4,3,2,1,0:T(8,128)}), f32[8,4,2,16,224]{4,3,2,1,0:T(8,128)}, u32[]{:S(2)}, u32[]{:S(2)}) async-start(f32[8,4,2,16,224]{4,3,2,1,0:T(8,128)} %broadcast_in_dim.26), calls=%async_computation.2 | async-start | bytes 2097152 | tf_op jit(solution)/shard_map/all_to_all | solution.py:14
  324.7 71.6 %all-reduce.17.cloned.1.call-start = ((), (), s32[]{:S(2)}) async-start(), calls=%async_computation.14 | async-start | bytes 1966080 | tf_op jit(solution)/shard_map/psum | solution.py:58
  341.2 55.2 %copy-start.9 = (f32[4,16,64]{2,1,0:T(8,128)S(1)}, f32[4,16,64]{2,1,0:T(8,128)}, u32[]{:S(2)}) copy-start(f32[4,16,64]{2,1,0:T(8,128)} %reduce_sum.233) | copy-start | bytes 49156
  342.3 189.8 %all-reduce.13.cloned.1.call-start = ((), (), s32[]{:S(2)}) async-start(), calls=%async_computation.12 | async-start | bytes 1966080 | tf_op jit(solution)/shard_map/psum | solution.py:59
  532.0 34.8 %copy-start.6 = (f32[4,2,16,512]{3,2,1,0:T(8,128)S(1)}, f32[4,2,16,512]{3,2,1,0:T(8,128)}, u32[]{:S(2)}) copy-start(f32[4,2,16,512]{3,2,1,0:T(8,128)} %get-tuple-element.14) | copy-start | bytes 786436
  532.0 39.3 %copy-start.5 = (f32[4,2,16,512]{3,2,1,0:T(8,128)S(1)}, f32[4,2,16,512]{3,2,1,0:T(8,128)}, u32[]{:S(2)}) copy-start(f32[4,2,16,512]{3,2,1,0:T(8,128)} %get-tuple-element.12) | copy-start | bytes 786436
  533.9 19.2 %all-to-all-start.7 = ((f32[8,4,1,16]{3,2,1,0:T(1,128)}), f32[8,4,1,16]{3,2,1,0:T(1,128)S(1)}, u32[]{:S(2)}, u32[]{:S(2)}) async-start(f32[8,4,1,16]{3,2,1,0:T(1,128)} %broadcast_in_dim.31), calls=%async_computation.7 | async-start | bytes 32768 | tf_op jit(solution)/shard_map/all_to_all | solution.py:14
  553.1 8.5 %all-to-all-start.11 = ((f32[8,1,128]{2,1,0:T(1,128)}), f32[8,1,128]{2,1,0:T(1,128)S(1)}, u32[]{:S(2)}, u32[]{:S(2)}) async-start(f32[8,1,128]{2,1,0:T(1,128)} %reshape.207), calls=%async_computation.11 | async-start | bytes 8192 | tf_op jit(solution)/shard_map/all_to_all | solution.py:14
  561.6 8.5 %all-to-all-start.3 = ((f32[8,1,128]{2,1,0:T(1,128)}), f32[8,1,128]{2,1,0:T(1,128)S(1)}, u32[]{:S(2)}, u32[]{:S(2)}) async-start(f32[8,1,128]{2,1,0:T(1,128)} %reshape.195), calls=%async_computation.3 | async-start | bytes 8192 | tf_op jit(solution)/shard_map/all_to_all | solution.py:14
Sparse Core Ops, SparseCore 0:
  60.9 57.8 all-reduce.18
  121.3 133.2 all-reduce.14
  342.4 53.8 all-reduce.16
  398.7 133.2 all-reduce.12
